TPU v7x, 32 devices: a whole 2x2x4 slice. The times are simulated.
32 devices in a mesh: expert: 4 (over y, core), shard: 8 (over z, x).
Axes of the slice: x: 2, y: 2, z: 4, core: 2. Of those that a mesh axis runs over, the one named last changes fastest.
Arguments:
- master_gate: float32 [128, 2048, 768], P('expert', 'shard'), may hold values from -0.125 to 0.125
- second_gate: bfloat16 [128, 2048, 768], P('expert', 'shard'), may hold values from -0.0625 to 0.0625
- master_up: float32 [128, 2048, 768], P('expert', 'shard'), may hold values from -0.125 to 0.125
- second_up: bfloat16 [128, 2048, 768], P('expert', 'shard'), may hold values from -0.0625 to 0.0625
- router_weight: float32 [2048, 128], P('shard', 'expert'), may hold values from -0.125 to 0.125
- router_gain: float32 [2048], P('shard'), may hold values from 0.25 to 1.75
Outputs:
- final_gate: bfloat16 [128, 768, 2048], P('expert', 'shard')
- final_up: bfloat16 [128, 768, 2048], P('expert', 'shard')
- serve_router: bfloat16 [2048, 128], replicated
All inputs are finite; a program needn't handle non-finite values.
Results may differ from a plain program's by a relative error of at most 0.001.
Values may be sent and summed in bfloat16 or wider, within the bound.
A program may use at most 192 MiB of HBM per device.

v0:
```python
import functools

import jax
import jax.numpy as jnp
from jax import lax
from jax.experimental import pallas as pl
from jax.experimental.pallas import tpu as pltpu
from jax.sharding import PartitionSpec as P

SLOTS = 12
LOADS = 2
MESH_IDS = pl.DeviceIdType.MESH


def plain(master_gate, second_gate, master_up, second_up, router_weight, router_gain):
    merged_gate = master_gate + second_gate.astype(jnp.float32)
    merged_up = master_up + second_up.astype(jnp.float32)
    narrow_gate, narrow_up = (merged_gate.astype(jnp.bfloat16), merged_up.astype(jnp.bfloat16))
    final_gate, final_up = (
        lax.all_to_all(narrow_gate, "shard", split_axis=2, concat_axis=1, tiled=True),
        lax.all_to_all(narrow_up, "shard", split_axis=2, concat_axis=1, tiled=True),
    )
    final_gate = jnp.transpose(final_gate, (0, 2, 1))
    final_up = jnp.transpose(final_up, (0, 2, 1))
    part_router = (router_weight * router_gain[:, None]).astype(jnp.bfloat16)
    row_router = lax.all_gather(part_router, "shard", axis=0, tiled=True)
    serve_router = lax.all_gather(row_router, "expert", axis=1, tiled=True)
    return (final_gate, final_up, serve_router)


def peers(me, n):
    half = n // 2
    mine, place = me // half, me % half
    far = [(1 - mine) * half + (place + i) % half for i in range(half)]
    near = [mine * half + (place + i) % half for i in range(1, half)]
    return far, near


def regroup_kernel(n, groups, mg, sg, mu, su, rw, gain, og, ou, orr,
                   in_m, in_s, stage, rw_v, gain_v, r_part, r_all,
                   load_m, load_s, load_r, send, own, recv, r_send, r_recv, f_send, f_recv):
    experts, rows, inner = mg.shape
    part = inner // n
    r_cols = rw.shape[0]
    group, me = lax.axis_index("expert"), lax.axis_index("shard")
    far, near = peers(me, n)
    to = far + near
    other = [(group + i) % groups for i in range(1, groups)]
    masters, seconds, outs = (mg, mu), (sg, su), (og, ou)
    home = pl.ds(pl.multiple_of(me * rows, rows), rows)

    def loads(a, e):
        slot = e % LOADS
        return (
            pltpu.make_async_copy(masters[a].at[e], in_m.at[a, slot], load_m.at[a, slot]),
            pltpu.make_async_copy(seconds[a].at[e], in_s.at[a, slot], load_s.at[a, slot]),
        )

    def start_loads(a, e):
        for copy in loads(a, e):
            copy.start()

    def router_loads():
        return (
            pltpu.make_async_copy(rw, rw_v, load_r.at[0]),
            pltpu.make_async_copy(gain, gain_v, load_r.at[1]),
        )

    def block(a, e, device):
        src = pl.ds(pl.multiple_of(device * part, part), part)
        return stage.at[a, e % SLOTS, src, :], outs[a].at[e, :, home]

    def start_sends(a, e):
        for device in to:
            src, dst = block(a, e, device)
            pltpu.make_async_remote_copy(
                src_ref=src, dst_ref=dst, send_sem=send.at[a, e % SLOTS], recv_sem=recv.at[a, e],
                device_id=(group, device), device_id_type=MESH_IDS,
            ).start()
        src, dst = block(a, e, me)
        pltpu.make_async_copy(src, dst, own.at[a, e % SLOTS]).start()

    def wait_sends(a, e):
        many = stage.at[a, e % SLOTS, pl.ds(0, (n - 1) * part), :]
        pltpu.make_async_copy(many, many, send.at[a, e % SLOTS]).wait()
        src, dst = block(a, e, me)
        pltpu.make_async_copy(src, dst, own.at[a, e % SLOTS]).wait()

    def merge(a, e):
        for copy in loads(a, e):
            copy.wait()

        @pl.when(e >= SLOTS)
        def _():
            wait_sends(a, e - SLOTS)

        slot, into = e % LOADS, e % SLOTS
        for c in range(inner // 128):
            cols = slice(c * 128, (c + 1) * 128)
            merged = in_m[a, slot, :, cols] + in_s[a, slot, :, cols].astype(jnp.float32)
            stage[a, into, cols, :] = merged.T.astype(jnp.bfloat16)

        @pl.when(e + LOADS < experts)
        def _():
            start_loads(a, e + LOADS)

    for a in range(2):
        start_loads(a, 0)
    for copy in router_loads():
        copy.start()
    for e in range(1, LOADS):
        for a in range(2):
            start_loads(a, e)

    barrier = pltpu.get_barrier_semaphore()
    for device in to:
        pl.semaphore_signal(barrier, inc=1, device_id=(group, device), device_id_type=MESH_IDS)
    for g in other:
        pl.semaphore_signal(barrier, inc=1, device_id=(g, me), device_id_type=MESH_IDS)

    merge(0, 0)
    for copy in router_loads():
        copy.wait()
    mine = (rw_v[...] * gain_v[...]).astype(jnp.bfloat16)
    r_rows = pl.ds(pl.multiple_of(group * r_cols, r_cols), r_cols)
    r_part[...] = mine
    r_all[r_rows, home] = mine
    pl.semaphore_wait(barrier, len(to) + len(other))
    start_sends(0, 0)
    merge(1, 0)

    def hand(src, dst, i, device):
        pltpu.make_async_remote_copy(
            src_ref=src, dst_ref=dst, send_sem=r_send.at[i], recv_sem=r_recv.at[i],
            device_id=(group, device), device_id_type=MESH_IDS,
        ).start()

    def wait_hands(sems, i, count):
        many = r_all.at[pl.ds(0, r_cols), pl.ds(0, count * rows)]
        pltpu.make_async_copy(many, many, sems.at[i]).wait()

    hand(r_part, r_all.at[r_rows, home], 0, far[0])
    for device in near:
        hand(r_part, r_all.at[r_rows, home], 1, device)

    def step(e, carry):
        merge(0, e)
        start_sends(1, e - 1)
        merge(1, e)
        start_sends(0, e)
        return carry

    lax.fori_loop(1, experts, step, 0)

    wait_hands(r_recv, 0, 1)
    mirror = r_all.at[r_rows, pl.ds(pl.multiple_of(far[0] * rows, rows), rows)]
    for device in near:
        hand(mirror, mirror, 2, device)
    start_sends(1, experts - 1)
    wait_hands(r_send, 0, 1)
    for i in (1, 2):
        wait_hands(r_recv, i, len(near))
        wait_hands(r_send, i, len(near))
    for g in other:
        pltpu.make_async_remote_copy(
            src_ref=r_all.at[r_rows, :], dst_ref=r_all.at[r_rows, :], send_sem=f_send, recv_sem=f_recv,
            device_id=(g, me), device_id_type=MESH_IDS,
        ).start()
    many = r_all.at[pl.ds(0, (groups - 1) * r_cols), :]
    pltpu.make_async_copy(many, many, f_recv).wait()
    pltpu.make_async_copy(many, many, f_send).wait()
    for c in range(orr.shape[0] // 128):
        span = slice(c * 128, (c + 1) * 128)
        orr[span, :] = r_all[:, span].astype(jnp.float32).T.astype(jnp.bfloat16)

    def drain(e, carry):
        for a in range(2):
            wait_sends(a, e)
        return carry

    lax.fori_loop(max(experts - SLOTS, 0), experts, drain, 0)

    def arrive(e, carry):
        for a in range(2):
            many = outs[a].at[e, :, pl.ds(0, (n - 1) * rows)]
            pltpu.make_async_copy(many, many, recv.at[a, e]).wait()
        return carry

    lax.fori_loop(0, experts, arrive, 0)


PIECES = 4


def put_kernel(gate, up, router, og, ou, orr, done, done_router):
    size = gate.shape[0] // PIECES
    copies = [
        pltpu.make_async_copy(src.at[pl.ds(i * size, size)], dst.at[pl.ds(i * size, size)], done.at[a, i])
        for i in range(PIECES)
        for a, (src, dst) in enumerate(((gate, og), (up, ou)))
    ]
    copies.append(pltpu.make_async_copy(router, orr, done_router))
    for copy in copies:
        copy.start()
    for copy in copies:
        copy.wait()


def put(*held):
    anywhere = pl.BlockSpec(memory_space=pl.ANY)
    return pl.pallas_call(
        put_kernel,
        out_shape=tuple(pltpu.HBM(x.shape, x.dtype) for x in held),
        in_specs=[anywhere] * len(held),
        out_specs=(anywhere,) * len(held),
        scratch_shapes=[pltpu.SemaphoreType.DMA((2, PIECES)), pltpu.SemaphoreType.DMA],
        compiler_params=pltpu.CompilerParams(vmem_limit_bytes=1024 * 1024),
        name="put",
    )(*held)


def fused(n, groups, master_gate, second_gate, master_up, second_up, router_weight, router_gain):
    experts, rows, inner = master_gate.shape
    r_cols = router_weight.shape[1]
    final = (experts, inner // n, rows * n)
    anywhere = pl.BlockSpec(memory_space=pl.ANY)
    dma = pltpu.SemaphoreType.DMA
    return put(*pl.pallas_call(
        functools.partial(regroup_kernel, n, groups),
        out_shape=(
            pltpu.VMEM(final, jnp.bfloat16),
            pltpu.VMEM(final, jnp.bfloat16),
            jax.ShapeDtypeStruct((rows * n, r_cols * groups), jnp.bfloat16),
        ),
        in_specs=[anywhere] * 6,
        out_specs=(anywhere, anywhere, pl.BlockSpec(memory_space=pltpu.VMEM)),
        scratch_shapes=[
            pltpu.VMEM((2, LOADS, rows, inner), jnp.float32),
            pltpu.VMEM((2, LOADS, rows, inner), jnp.bfloat16),
            pltpu.VMEM((2, SLOTS, inner, rows), jnp.bfloat16),
            pltpu.VMEM((r_cols, rows), jnp.float32),
            pltpu.VMEM((1, rows), jnp.float32),
            pltpu.VMEM((r_cols, rows), jnp.bfloat16),
            pltpu.VMEM((r_cols * groups, rows * n), jnp.bfloat16),
            dma((2, LOADS)), dma((2, LOADS)), dma((2,)),
            dma((2, SLOTS)), dma((2, SLOTS)), dma((2, experts)),
            dma((3,)), dma((3,)), dma, dma,
        ],
        compiler_params=pltpu.CompilerParams(
            collective_id=0, has_side_effects=True, vmem_limit_bytes=24 * 1024 * 1024,
        ),
        name="regroup",
    )(
        master_gate, second_gate, master_up, second_up,
        pltpu.with_memory_space_constraint(router_weight.T, pltpu.HBM),
        pltpu.with_memory_space_constraint(router_gain[None, :], pltpu.HBM),
    ))


def solution(mesh):
    n, groups = mesh.shape["shard"], mesh.shape["expert"]

    def shards(*args):
        experts, rows, inner = args[0].shape
        r_cols = args[4].shape[1]
        fits = (
            n % 2 == 0 and n > 2 and groups > 1 and rows % 128 == 0 and inner % 128 == 0
            and (inner // n) % 16 == 0 and r_cols % 16 == 0 and experts % PIECES == 0 and experts >= max(SLOTS, LOADS)
        )
        return fused(n, groups, *args) if fits else plain(*args)

    in_specs = (
        P("expert", "shard", None),
        P("expert", "shard", None),
        P("expert", "shard", None),
        P("expert", "shard", None),
        P("shard", "expert"),
        P("shard"),
    )
    out_specs = (P("expert", "shard", None), P("expert", "shard", None), P())
    return jax.shard_map(shards, mesh=mesh, in_specs=in_specs, out_specs=out_specs, check_vma=False)
```

profile of v0, /device:TPU:0, one launch (start us, length us, event | category | flops | bytes accessed | tf_op | source)
XLA Modules:
  0.0 558.0 jit_solution(17747065503130065202)
XLA Ops:
  0.6 548.8 %regroup.1 = (bf16[32,96,2048]{2,1,0:T(8,128)(2,1)S(1)}, bf16[32,96,2048]{2,1,0:T(8,128)(2,1)S(1)}, bf16[2048,128]{1,0:T(8,128)(2,1)S(1)}) custom-call(f32[32,256,768]{2,1,0:T(8,128)} %mg.1, bf16[32,256,768]{2,1,0:T(8,128)(2,1)} %sg.1, f32[32,256,768]{2,1,0:T(8,128)} %mu.1, bf16[32,256,768]{2,1,0:T(8,128)(2,1)} %su.1, f32[32,256]{1,0:T(8,128)} %bitcast.2, ...), custom_call_target="tpu_custom_call" | custom-call | tf_op jit(solution)/shard_map/regroup/pallas_call | solution.py:228
  549.4 8.6 %put.1 = (bf16[32,96,2048]{2,1,0:T(8,128)(2,1)}, bf16[32,96,2048]{2,1,0:T(8,128)(2,1)}, bf16[2048,128]{1,0:T(8,128)(2,1)}) custom-call(bf16[32,96,2048]{2,1,0:T(8,128)(2,1)S(1)} %get-tuple-element.6.gate, bf16[32,96,2048]{2,1,0:T(8,128)(2,1)S(1)} %get-tuple-element.7.up, bf16[2048,128]{1,0:T(8,128)(2,1)S(1)} %get-tuple-element.8.router), custom_call_target="tpu_custom_call" | custom-call | tf_op jit(solution)/shard_map/put/pallas_call | solution.py:211
where the time goes:
time: 558 us
  Pallas kernels  557 us (100%)
    pallas_call x1, Pallas kernels, fused(): pl.pallas_call(functools.partial(regroup_kernel, n, groups), out_shape=(p...  549 us

commit v1 on v0

--- a/solution.py
+++ b/solution.py
@@ -9,6 +9,8 @@
 
 SLOTS = 12
 LOADS = 2
+SECOND = 4
+HELD = 13
 MESH_IDS = pl.DeviceIdType.MESH
 
 
@@ -29,22 +31,27 @@
 
 
 def peers(me, n):
-    half = n // 2
-    mine, place = me // half, me % half
-    far = [(1 - mine) * half + (place + i) % half for i in range(half)]
+    half, quarter = n // 2, n // 4
+    mine, place, x = me // half, me % half, me % quarter
+    is_end = (place // quarter) == mine
+    far_end = [(1 - mine) * (n - quarter) + (x + i) % quarter for i in range(quarter)]
+    far_mid = [half - mine * quarter + (x + i) % quarter for i in range(quarter)]
     near = [mine * half + (place + i) % half for i in range(1, half)]
-    return far, near
-
-
-def regroup_kernel(n, groups, mg, sg, mu, su, rw, gain, og, ou, orr,
+    return is_end, far_end, far_mid, near
+
+
+def regroup_kernel(n, groups, mg, sg, mu, su, rw, gain, og, ou, orr, stash,
                    in_m, in_s, stage, rw_v, gain_v, r_part, r_all,
                    load_m, load_s, load_r, send, own, recv, r_send, r_recv, f_send, f_recv):
     experts, rows, inner = mg.shape
     part = inner // n
     r_cols = rw.shape[0]
     group, me = lax.axis_index("expert"), lax.axis_index("shard")
-    far, near = peers(me, n)
-    to = far + near
+    is_end, far_end, far_mid, near = peers(me, n)
+    mirror_x = jnp.where(is_end, far_end[0], far_mid[0])
+    to = far_end + far_mid + near
+    quarter = n // 4
+    total = 2 * experts
     other = [(group + i) % groups for i in range(1, groups)]
     masters, seconds, outs = (mg, mu), (sg, su), (og, ou)
     home = pl.ds(pl.multiple_of(me * rows, rows), rows)
@@ -70,18 +77,35 @@
         src = pl.ds(pl.multiple_of(device * part, part), part)
         return stage.at[a, e % SLOTS, src, :], outs[a].at[e, :, home]
 
-    def start_sends(a, e):
-        for device in to:
+    def send_to(a, e, devices):
+        for device in devices:
             src, dst = block(a, e, device)
             pltpu.make_async_remote_copy(
                 src_ref=src, dst_ref=dst, send_sem=send.at[a, e % SLOTS], recv_sem=recv.at[a, e],
                 device_id=(group, device), device_id_type=MESH_IDS,
             ).start()
+
+    def seconds_of(a, e):
+        return is_end & (2 * e + a >= total - SECOND)
+
+    def start_sends(a, e):
+        m = 2 * e + a
+
+        @pl.when(~seconds_of(a, e))
+        def _():
+            send_to(a, e, far_end)
+
+        for i, device in enumerate(far_mid):
+            @pl.when(is_end | (m * quarter + i < total * quarter - HELD))
+            def _():
+                send_to(a, e, [device])
+
+        send_to(a, e, near)
         src, dst = block(a, e, me)
         pltpu.make_async_copy(src, dst, own.at[a, e % SLOTS]).start()
 
-    def wait_sends(a, e):
-        many = stage.at[a, e % SLOTS, pl.ds(0, (n - 1) * part), :]
+    def wait_sends(a, e, blocks=n - 1):
+        many = stage.at[a, e % SLOTS, pl.ds(0, blocks * part), :]
         pltpu.make_async_copy(many, many, send.at[a, e % SLOTS]).wait()
         src, dst = block(a, e, me)
         pltpu.make_async_copy(src, dst, own.at[a, e % SLOTS]).wait()
@@ -99,6 +123,11 @@
             cols = slice(c * 128, (c + 1) * 128)
             merged = in_m[a, slot, :, cols] + in_s[a, slot, :, cols].astype(jnp.float32)
             stage[a, into, cols, :] = merged.T.astype(jnp.bfloat16)
+
+        @pl.when(2 * e + a >= total - SECOND)
+        def _():
+            theirs = pl.ds(pl.multiple_of((1 - me // (n // 2)) * (n - quarter) * part, quarter * part), quarter * part)
+            stash[2 * e + a - (total - SECOND)] = stage[a, into, theirs, :]
 
         @pl.when(e + LOADS < experts)
         def _():
@@ -139,7 +168,7 @@
         many = r_all.at[pl.ds(0, r_cols), pl.ds(0, count * rows)]
         pltpu.make_async_copy(many, many, sems.at[i]).wait()
 
-    hand(r_part, r_all.at[r_rows, home], 0, far[0])
+    hand(r_part, r_all.at[r_rows, home], 0, mirror_x)
     for device in near:
         hand(r_part, r_all.at[r_rows, home], 1, device)
 
@@ -152,11 +181,18 @@
 
     lax.fori_loop(1, experts, step, 0)
 
+    start_sends(1, experts - 1)
+
+    @pl.when(~is_end)
+    def _():
+        for i in range(total * quarter - HELD, total * quarter):
+            m = i // quarter
+            send_to(m % 2, m // 2, [far_mid[i % quarter]])
+
     wait_hands(r_recv, 0, 1)
-    mirror = r_all.at[r_rows, pl.ds(pl.multiple_of(far[0] * rows, rows), rows)]
+    mirror = r_all.at[r_rows, pl.ds(pl.multiple_of(mirror_x * rows, rows), rows)]
     for device in near:
         hand(mirror, mirror, 2, device)
-    start_sends(1, experts - 1)
     wait_hands(r_send, 0, 1)
     for i in (1, 2):
         wait_hands(r_recv, i, len(near))
@@ -175,24 +211,113 @@
 
     def drain(e, carry):
         for a in range(2):
-            wait_sends(a, e)
+            @pl.when(seconds_of(a, e))
+            def _():
+                wait_sends(a, e, n - 1 - quarter)
+
+            @pl.when(~seconds_of(a, e))
+            def _():
+                wait_sends(a, e)
         return carry
 
     lax.fori_loop(max(experts - SLOTS, 0), experts, drain, 0)
+
+    def wait_recv(a, e, blocks):
+        many = outs[a].at[e, :, pl.ds(0, blocks * rows)]
+        pltpu.make_async_copy(many, many, recv.at[a, e]).wait()
 
     def arrive(e, carry):
         for a in range(2):
-            many = outs[a].at[e, :, pl.ds(0, (n - 1) * rows)]
-            pltpu.make_async_copy(many, many, recv.at[a, e]).wait()
+            @pl.when(seconds_of(a, e))
+            def _():
+                wait_recv(a, e, n - 1 - quarter)
+
+            @pl.when(~seconds_of(a, e))
+            def _():
+                wait_recv(a, e, n - 1)
         return carry
 
     lax.fori_loop(0, experts, arrive, 0)
 
 
+def second_kernel(n, stash, after, land, send, recv):
+    group, me = lax.axis_index("expert"), lax.axis_index("shard")
+    is_end, far_end, _, _ = peers(me, n)
+    quarter = n // 4
+    part, rows = stash.shape[1] // quarter, stash.shape[2]
+    x = me % quarter
+    barrier = pltpu.get_barrier_semaphore()
+
+    @pl.when(is_end)
+    def _():
+        for device in far_end:
+            pl.semaphore_signal(barrier, inc=1, device_id=(group, device), device_id_type=MESH_IDS)
+        pl.semaphore_wait(barrier, quarter)
+        for m in range(SECOND):
+            for device in far_end:
+                pltpu.make_async_remote_copy(
+                    src_ref=stash.at[m, pl.ds(pl.multiple_of(device % quarter * part, part), part), :],
+                    dst_ref=land.at[m, :, pl.ds(pl.multiple_of(x * rows, rows), rows)],
+                    send_sem=send, recv_sem=recv, device_id=(group, device), device_id_type=MESH_IDS,
+                ).start()
+        pltpu.make_async_copy(land, land, recv).wait()
+        pltpu.make_async_copy(stash, stash, send).wait()
+
+
+def second(n, stash, after):
+    _, span, rows = stash.shape
+    quarter = n // 4
+    anywhere = pl.BlockSpec(memory_space=pl.ANY)
+    return pl.pallas_call(
+        functools.partial(second_kernel, n),
+        out_shape=pltpu.VMEM((SECOND, span // quarter, quarter * rows), stash.dtype),
+        in_specs=[anywhere, anywhere],
+        out_specs=anywhere,
+        scratch_shapes=[pltpu.SemaphoreType.DMA, pltpu.SemaphoreType.DMA],
+        compiler_params=pltpu.CompilerParams(
+            collective_id=1, has_side_effects=True, vmem_limit_bytes=1024 * 1024,
+        ),
+        name="second",
+    )(stash, after)
+
+
+def fill_kernel(n, gate, up, land, og, ou, done):
+    me = lax.axis_index("shard")
+    is_end, _, _, _ = peers(me, n)
+    half, quarter = n // 2, n // 4
+    experts, width = gate.shape[0], land.shape[2]
+    spot = pl.ds(pl.multiple_of((1 - me // half) * (n - quarter) * (width // quarter), width), width)
+
+    @pl.when(is_end)
+    def _():
+        copies = []
+        for i in range(SECOND):
+            m = 2 * experts - SECOND + i
+            copies.append(pltpu.make_async_copy(land.at[i], (og, ou)[m % 2].at[m // 2, :, spot], done.at[i]))
+        for copy in copies:
+            copy.start()
+        for copy in copies:
+            copy.wait()
+
+
+def fill(n, gate, up, land):
+    anywhere = pl.BlockSpec(memory_space=pl.ANY)
+    return pl.pallas_call(
+        functools.partial(fill_kernel, n),
+        out_shape=tuple(pltpu.HBM(x.shape, x.dtype) for x in (gate, up)),
+        in_specs=[anywhere] * 3,
+        out_specs=(anywhere,) * 2,
+        scratch_shapes=[pltpu.SemaphoreType.DMA((SECOND,))],
+        input_output_aliases={0: 0, 1: 1},
+        compiler_params=pltpu.CompilerParams(vmem_limit_bytes=1024 * 1024),
+        name="fill",
+    )(gate, up, land)
+
+
 PIECES = 4
 
 
-def put_kernel(gate, up, router, og, ou, orr, done, done_router):
+def put_kernel(gate, up, router, og, ou, orr, after, done, done_router):
     size = gate.shape[0] // PIECES
     copies = [
         pltpu.make_async_copy(src.at[pl.ds(i * size, size)], dst.at[pl.ds(i * size, size)], done.at[a, i])
@@ -210,9 +335,9 @@
     anywhere = pl.BlockSpec(memory_space=pl.ANY)
     return pl.pallas_call(
         put_kernel,
-        out_shape=tuple(pltpu.HBM(x.shape, x.dtype) for x in held),
+        out_shape=tuple(pltpu.HBM(x.shape, x.dtype) for x in held) + (pltpu.VMEM((8, 128), jnp.float32),),
         in_specs=[anywhere] * len(held),
-        out_specs=(anywhere,) * len(held),
+        out_specs=(anywhere,) * (len(held) + 1),
         scratch_shapes=[pltpu.SemaphoreType.DMA((2, PIECES)), pltpu.SemaphoreType.DMA],
         compiler_params=pltpu.CompilerParams(vmem_limit_bytes=1024 * 1024),
         name="put",
@@ -225,15 +350,16 @@
     final = (experts, inner // n, rows * n)
     anywhere = pl.BlockSpec(memory_space=pl.ANY)
     dma = pltpu.SemaphoreType.DMA
-    return put(*pl.pallas_call(
+    *held, stash = pl.pallas_call(
         functools.partial(regroup_kernel, n, groups),
         out_shape=(
             pltpu.VMEM(final, jnp.bfloat16),
             pltpu.VMEM(final, jnp.bfloat16),
             jax.ShapeDtypeStruct((rows * n, r_cols * groups), jnp.bfloat16),
+            pltpu.VMEM((SECOND, inner // 4, rows), jnp.bfloat16),
         ),
         in_specs=[anywhere] * 6,
-        out_specs=(anywhere, anywhere, pl.BlockSpec(memory_space=pltpu.VMEM)),
+        out_specs=(anywhere, anywhere, pl.BlockSpec(memory_space=pltpu.VMEM), pl.BlockSpec(memory_space=pltpu.VMEM)),
         scratch_shapes=[
             pltpu.VMEM((2, LOADS, rows, inner), jnp.float32),
             pltpu.VMEM((2, LOADS, rows, inner), jnp.bfloat16),
@@ -254,7 +380,9 @@
         master_gate, second_gate, master_up, second_up,
         pltpu.with_memory_space_constraint(router_weight.T, pltpu.HBM),
         pltpu.with_memory_space_constraint(router_gain[None, :], pltpu.HBM),
-    ))
+    )
+    gate, up, router, after = put(*held)
+    return *fill(n, gate, up, second(n, stash, after)), router
 
 
 def solution(mesh):
@@ -264,8 +392,8 @@
         experts, rows, inner = args[0].shape
         r_cols = args[4].shape[1]
         fits = (
-            n % 2 == 0 and n > 2 and groups > 1 and rows % 128 == 0 and inner % 128 == 0
-            and (inner // n) % 16 == 0 and r_cols % 16 == 0 and experts % PIECES == 0 and experts >= max(SLOTS, LOADS)
+            n % 4 == 0 and groups > 1 and rows % 128 == 0 and inner % 128 == 0
+            and (inner // n) % 16 == 0 and r_cols % 16 == 0 and experts % PIECES == 0 and experts >= max(SLOTS, LOADS) and 2 * SLOTS * (n // 4) > HELD + n // 2
         )
         return fused(n, groups, *args) if fits else plain(*args)
 

time: 558 us -> 550 us (0.986)
  Pallas kernels: 557 us -> 550 us
    pallas_call x1, Pallas kernels: 549 us -> 528 us  [fused(): pl.pallas_call(functools.partial(regroup_kernel, n, groups), out_shape=(p...]
    pallas_call x0 -> x2, Pallas kernels: none -> 13 us  [the longest x1 12.2 us: second(): pl.pallas_call(functools.partial(second_kernel, n), out_shape=pltpu.VMEM(...]
where the time goes in v1:
time: 550 us
  Pallas kernels  550 us (100%)
    pallas_call x1, Pallas kernels, fused(): pl.pallas_call(functools.partial(regroup_kernel, n, groups), out_shape=(p...  528 us
    pallas_call x1, Pallas kernels, second(): pl.pallas_call(functools.partial(second_kernel, n), out_shape=pltpu.VMEM(...  12.2 us

profile of v1, /device:TPU:0, one launch (start us, length us, event | category | flops | bytes accessed | tf_op | source)
XLA Modules:
  0.0 550.2 jit_solution(16152760443767085047)
XLA Ops:
  0.6 527.9 %regroup.1 = (bf16[32,96,2048]{2,1,0:T(8,128)(2,1)S(1)}, bf16[32,96,2048]{2,1,0:T(8,128)(2,1)S(1)}, bf16[2048,128]{1,0:T(8,128)(2,1)S(1)}, bf16[4,192,256]{2,1,0:T(8,128)(2,1)S(1)}) custom-call(f32[32,256,768]{2,1,0:T(8,128)} %mg.1, bf16[32,256,768]{2,1,0:T(8,128)(2,1)} %sg.1, f32[32,256,768]{2,1,0:T(8,128)} %mu.1, bf16[32,256,768]{2,1,0:T(8,128)(2,1)} %su.1, ...), custom_call_target="tpu_custom_call" | custom-call | tf_op jit(solution)/shard_map/regroup/pallas_call | solution.py:353
  528.5 8.6 %put.1 = (bf16[32,96,2048]{2,1,0:T(8,128)(2,1)}, bf16[32,96,2048]{2,1,0:T(8,128)(2,1)}, bf16[2048,128]{1,0:T(8,128)(2,1)}, f32[8,128]{1,0:T(8,128)S(1)}) custom-call(bf16[32,96,2048]{2,1,0:T(8,128)(2,1)S(1)} %get-tuple-element.13.gate, bf16[32,96,2048]{2,1,0:T(8,128)(2,1)S(1)} %get-tuple-element.14.up, bf16[2048,128]{1,0:T(8,128)(2,1)S(1)} %get-tuple-element.15.router), custom_call_target="tpu_custom_call" | custom-call | tf_op jit(solution)/shard_map/put/pallas_call | solution.py:336
  537.2 12.2 %second.1.land = bf16[4,96,512]{2,1,0:T(8,128)(2,1)S(1)} custom-call(bf16[4,192,256]{2,1,0:T(8,128)(2,1)S(1)} %get-tuple-element.18.stash, f32[8,128]{1,0:T(8,128)S(1)} %get-tuple-element.19.after), custom_call_target="tpu_custom_call" | custom-call | tf_op jit(solution)/shard_map/second/pallas_call | solution.py:271
  549.4 0.8 fill.1

commit v2 on v1

--- a/solution.py
+++ b/solution.py
@@ -10,7 +10,8 @@
 SLOTS = 12
 LOADS = 2
 SECOND = 4
-HELD = 13
+HELD = (13, 12)
+EARLY = 4
 MESH_IDS = pl.DeviceIdType.MESH
 
 
@@ -32,26 +33,29 @@
 
 def peers(me, n):
     half, quarter = n // 2, n // 4
-    mine, place, x = me // half, me % half, me % quarter
+    mine, place = me // half, me % half
     is_end = (place // quarter) == mine
-    far_end = [(1 - mine) * (n - quarter) + (x + i) % quarter for i in range(quarter)]
-    far_mid = [half - mine * quarter + (x + i) % quarter for i in range(quarter)]
+    far_end = [(1 - mine) * (n - quarter) + i for i in range(quarter)]
+    far_mid = [half - mine * quarter + i for i in range(quarter)]
     near = [mine * half + (place + i) % half for i in range(1, half)]
     return is_end, far_end, far_mid, near
 
 
 def regroup_kernel(n, groups, mg, sg, mu, su, rw, gain, og, ou, orr, stash,
                    in_m, in_s, stage, rw_v, gain_v, r_part, r_all,
-                   load_m, load_s, load_r, send, own, recv, r_send, r_recv, f_send, f_recv):
+                   load_m, load_s, load_r, send, own, recv, r_send, r_recv, f_send, f_recv, known, crossed, all_known):
     experts, rows, inner = mg.shape
     part = inner // n
     r_cols = rw.shape[0]
     group, me = lax.axis_index("expert"), lax.axis_index("shard")
     is_end, far_end, far_mid, near = peers(me, n)
-    mirror_x = jnp.where(is_end, far_end[0], far_mid[0])
-    to = far_end + far_mid + near
-    quarter = n // 4
+    half, quarter = n // 2, n // 4
+    mine, x = me // half, me % quarter
+    mirror_x = jnp.where(is_end, far_end[0], far_mid[0]) + x
+    near_mid = half - (1 - mine) * quarter + x
+    near_end = mine * (n - quarter)
     total = 2 * experts
+    held = jnp.where(group % 2 == 0, HELD[0], HELD[1])
     other = [(group + i) % groups for i in range(1, groups)]
     masters, seconds, outs = (mg, mu), (sg, su), (og, ou)
     home = pl.ds(pl.multiple_of(me * rows, rows), rows)
@@ -88,7 +92,7 @@
     def seconds_of(a, e):
         return is_end & (2 * e + a >= total - SECOND)
 
-    def start_sends(a, e):
+    def start_sends(a, e, early=False):
         m = 2 * e + a
 
         @pl.when(~seconds_of(a, e))
@@ -96,7 +100,7 @@
             send_to(a, e, far_end)
 
         for i, device in enumerate(far_mid):
-            @pl.when(is_end | (m * quarter + i < total * quarter - HELD))
+            @pl.when(is_end | (x != i if early else m * quarter + i < total * quarter - held))
             def _():
                 send_to(a, e, [device])
 
@@ -126,7 +130,7 @@
 
         @pl.when(2 * e + a >= total - SECOND)
         def _():
-            theirs = pl.ds(pl.multiple_of((1 - me // (n // 2)) * (n - quarter) * part, quarter * part), quarter * part)
+            theirs = pl.ds(pl.multiple_of(far_end[0] * part, quarter * part), quarter * part)
             stash[2 * e + a - (total - SECOND)] = stage[a, into, theirs, :]
 
         @pl.when(e + LOADS < experts)
@@ -142,21 +146,63 @@
             start_loads(a, e)
 
     barrier = pltpu.get_barrier_semaphore()
-    for device in to:
+
+    def greet(group, device):
         pl.semaphore_signal(barrier, inc=1, device_id=(group, device), device_id_type=MESH_IDS)
-    for g in other:
-        pl.semaphore_signal(barrier, inc=1, device_id=(g, me), device_id_type=MESH_IDS)
-
-    merge(0, 0)
-    for copy in router_loads():
-        copy.wait()
-    mine = (rw_v[...] * gain_v[...]).astype(jnp.bfloat16)
+
+    def tell(flag, group, device):
+        pl.semaphore_signal(flag, inc=1, device_id=(group, device), device_id_type=MESH_IDS)
+
+    @pl.when(is_end)
+    def _():
+        for device in far_end:
+            greet(group, device)
+        for i in range(1, quarter):
+            greet(group, near_end + (x + i) % quarter)
+        for g in other:
+            greet(g, me)
+
+    @pl.when(~is_end)
+    def _():
+        greet(group, mirror_x)
+        pl.semaphore_wait(barrier, 1)
+        for device in far_end:
+            greet(group, device)
+        for i in range(quarter):
+            greet(group, near_end + (x + i) % quarter)
+
+    def send_early(a, e):
+        @pl.when(~is_end)
+        def _():
+            send_to(a, e, [mirror_x])
+
     r_rows = pl.ds(pl.multiple_of(group * r_cols, r_cols), r_cols)
-    r_part[...] = mine
-    r_all[r_rows, home] = mine
-    pl.semaphore_wait(barrier, len(to) + len(other))
-    start_sends(0, 0)
-    merge(1, 0)
+    for m in range(EARLY):
+        merge(m % 2, m // 2)
+        if m == 0:
+            for copy in router_loads():
+                copy.wait()
+            weight = (rw_v[...] * gain_v[...]).astype(jnp.bfloat16)
+            r_part[...] = weight
+            r_all[r_rows, home] = weight
+            send_early(0, 0)
+        if m == 1:
+            @pl.when(is_end)
+            def _():
+                pl.semaphore_wait(barrier, n - 1 + len(other))
+                tell(known, group, near_mid)
+                for g in other:
+                    tell(crossed, g, me)
+        if m > 1:
+            send_early((m - 1) % 2, (m - 1) // 2)
+    send_early((EARLY - 1) % 2, (EARLY - 1) // 2)
+
+    @pl.when(~is_end)
+    def _():
+        pl.semaphore_wait(known, 1)
+
+    for m in range(EARLY):
+        start_sends(m % 2, m // 2, early=True)
 
     def hand(src, dst, i, device):
         pltpu.make_async_remote_copy(
@@ -171,6 +217,10 @@
     hand(r_part, r_all.at[r_rows, home], 0, mirror_x)
     for device in near:
         hand(r_part, r_all.at[r_rows, home], 1, device)
+
+    merge(0, EARLY // 2)
+    merge(1, EARLY // 2)
+    start_sends(0, EARLY // 2)
 
     def step(e, carry):
         merge(0, e)
@@ -179,15 +229,18 @@
         start_sends(0, e)
         return carry
 
-    lax.fori_loop(1, experts, step, 0)
+    lax.fori_loop(EARLY // 2 + 1, experts, step, 0)
 
     start_sends(1, experts - 1)
 
     @pl.when(~is_end)
     def _():
-        for i in range(total * quarter - HELD, total * quarter):
+        for i in range(total * quarter - max(HELD), total * quarter):
             m = i // quarter
-            send_to(m % 2, m // 2, [far_mid[i % quarter]])
+
+            @pl.when(i >= total * quarter - held)
+            def _():
+                send_to(m % 2, m // 2, [far_mid[i % quarter]])
 
     wait_hands(r_recv, 0, 1)
     mirror = r_all.at[r_rows, pl.ds(pl.multiple_of(mirror_x * rows, rows), rows)]
@@ -197,6 +250,15 @@
     for i in (1, 2):
         wait_hands(r_recv, i, len(near))
         wait_hands(r_send, i, len(near))
+    @pl.when(is_end)
+    def _():
+        pl.semaphore_wait(crossed, len(other))
+        tell(all_known, group, near_mid)
+
+    @pl.when(~is_end)
+    def _():
+        pl.semaphore_wait(all_known, 1)
+
     for g in other:
         pltpu.make_async_remote_copy(
             src_ref=r_all.at[r_rows, :], dst_ref=r_all.at[r_rows, :], send_sem=f_send, recv_sem=f_recv,
@@ -253,13 +315,14 @@
         for device in far_end:
             pl.semaphore_signal(barrier, inc=1, device_id=(group, device), device_id_type=MESH_IDS)
         pl.semaphore_wait(barrier, quarter)
-        for m in range(SECOND):
-            for device in far_end:
-                pltpu.make_async_remote_copy(
-                    src_ref=stash.at[m, pl.ds(pl.multiple_of(device % quarter * part, part), part), :],
-                    dst_ref=land.at[m, :, pl.ds(pl.multiple_of(x * rows, rows), rows)],
-                    send_sem=send, recv_sem=recv, device_id=(group, device), device_id_type=MESH_IDS,
-                ).start()
+        for i in range(quarter * SECOND):
+            to, m = i // SECOND, i % SECOND
+            pltpu.make_async_remote_copy(
+                src_ref=stash.at[m, pl.ds(to * part, part), :],
+                dst_ref=land.at[m, :, pl.ds(pl.multiple_of(x * rows, rows), rows)],
+                send_sem=send, recv_sem=recv,
+                device_id=(group, far_end[to]), device_id_type=MESH_IDS,
+            ).start()
         pltpu.make_async_copy(land, land, recv).wait()
         pltpu.make_async_copy(stash, stash, send).wait()
 
@@ -349,7 +412,7 @@
     r_cols = router_weight.shape[1]
     final = (experts, inner // n, rows * n)
     anywhere = pl.BlockSpec(memory_space=pl.ANY)
-    dma = pltpu.SemaphoreType.DMA
+    dma, regular = pltpu.SemaphoreType.DMA, pltpu.SemaphoreType.REGULAR
     *held, stash = pl.pallas_call(
         functools.partial(regroup_kernel, n, groups),
         out_shape=(
@@ -371,6 +434,7 @@
             dma((2, LOADS)), dma((2, LOADS)), dma((2,)),
             dma((2, SLOTS)), dma((2, SLOTS)), dma((2, experts)),
             dma((3,)), dma((3,)), dma, dma,
+            regular, regular, regular,
         ],
         compiler_params=pltpu.CompilerParams(
             collective_id=0, has_side_effects=True, vmem_limit_bytes=24 * 1024 * 1024,
@@ -393,7 +457,7 @@
         r_cols = args[4].shape[1]
         fits = (
             n % 4 == 0 and groups > 1 and rows % 128 == 0 and inner % 128 == 0
-            and (inner // n) % 16 == 0 and r_cols % 16 == 0 and experts % PIECES == 0 and experts >= max(SLOTS, LOADS) and 2 * SLOTS * (n // 4) > HELD + n // 2
+            and (inner // n) % 16 == 0 and r_cols % 16 == 0 and experts % PIECES == 0 and experts > max(SLOTS, LOADS, EARLY) and 2 * SLOTS * (n // 4) > max(HELD) + n // 2
         )
         return fused(n, groups, *args) if fits else plain(*args)
 

time: 550 us -> 548 us (level)
  no operation moved by 1% of the time
where the time goes in v2:
time: 548 us; the launch traced here: 547 us
  Pallas kernels  546 us (100%)
    pallas_call x1, Pallas kernels, fused(): pl.pallas_call(functools.partial(regroup_kernel, n, groups), out_shape=(p...  526 us

profile of v2, /device:TPU:0, one launch (start us, length us, event | category | flops | bytes accessed | tf_op | source)
XLA Modules:
  0.0 547.1 jit_solution(4119601208269280326)
XLA Ops:
  0.6 526.3 %regroup.1 = (bf16[32,96,2048]{2,1,0:T(8,128)(2,1)S(1)}, bf16[32,96,2048]{2,1,0:T(8,128)(2,1)S(1)}, bf16[2048,128]{1,0:T(8,128)(2,1)S(1)}, bf16[4,192,256]{2,1,0:T(8,128)(2,1)S(1)}) custom-call(f32[32,256,768]{2,1,0:T(8,128)} %mg.1, bf16[32,256,768]{2,1,0:T(8,128)(2,1)} %sg.1, f32[32,256,768]{2,1,0:T(8,128)} %mu.1, bf16[32,256,768]{2,1,0:T(8,128)(2,1)} %su.1, ...), custom_call_target="tpu_custom_call" | custom-call | tf_op jit(solution)/shard_map/regroup/pallas_call | solution.py:416
  527.0 8.6 %put.1 = (bf16[32,96,2048]{2,1,0:T(8,128)(2,1)}, bf16[32,96,2048]{2,1,0:T(8,128)(2,1)}, bf16[2048,128]{1,0:T(8,128)(2,1)}, f32[8,128]{1,0:T(8,128)S(1)}) custom-call(bf16[32,96,2048]{2,1,0:T(8,128)(2,1)S(1)} %get-tuple-element.13.gate, bf16[32,96,2048]{2,1,0:T(8,128)(2,1)S(1)} %get-tuple-element.14.up, bf16[2048,128]{1,0:T(8,128)(2,1)S(1)} %get-tuple-element.15.router), custom_call_target="tpu_custom_call" | custom-call | tf_op jit(solution)/shard_map/put/pallas_call | solution.py:399
  535.6 10.7 %second.1.land = bf16[4,96,512]{2,1,0:T(8,128)(2,1)S(1)} custom-call(bf16[4,192,256]{2,1,0:T(8,128)(2,1)S(1)} %get-tuple-element.18.stash, f32[8,128]{1,0:T(8,128)S(1)} %get-tuple-element.19.after), custom_call_target="tpu_custom_call" | custom-call | tf_op jit(solution)/shard_map/second/pallas_call | solution.py:334
  546.3 0.8 fill.1

commit v3 on v2

--- a/solution.py
+++ b/solution.py
@@ -9,9 +9,10 @@
 
 SLOTS = 12
 LOADS = 2
-SECOND = 4
+ENDS = 6
+MIDS = 1
 HELD = (13, 12)
-EARLY = 4
+EARLY = 8
 MESH_IDS = pl.DeviceIdType.MESH
 
 
@@ -90,17 +91,17 @@
             ).start()
 
     def seconds_of(a, e):
-        return is_end & (2 * e + a >= total - SECOND)
+        return 2 * e + a >= total - jnp.where(is_end, ENDS, MIDS)
 
     def start_sends(a, e, early=False):
         m = 2 * e + a
 
-        @pl.when(~seconds_of(a, e))
+        @pl.when(~is_end | (m < total - ENDS))
         def _():
             send_to(a, e, far_end)
 
         for i, device in enumerate(far_mid):
-            @pl.when(is_end | (x != i if early else m * quarter + i < total * quarter - held))
+            @pl.when(is_end | (x != i if early else m * quarter + i < (total - MIDS) * quarter - held))
             def _():
                 send_to(a, e, [device])
 
@@ -128,10 +129,10 @@
             merged = in_m[a, slot, :, cols] + in_s[a, slot, :, cols].astype(jnp.float32)
             stage[a, into, cols, :] = merged.T.astype(jnp.bfloat16)
 
-        @pl.when(2 * e + a >= total - SECOND)
+        @pl.when(2 * e + a >= total - ENDS)
         def _():
-            theirs = pl.ds(pl.multiple_of(far_end[0] * part, quarter * part), quarter * part)
-            stash[2 * e + a - (total - SECOND)] = stage[a, into, theirs, :]
+            theirs = pl.ds(pl.multiple_of(jnp.where(is_end, far_end[0], far_mid[0]) * part, quarter * part), quarter * part)
+            stash[2 * e + a - (total - ENDS)] = stage[a, into, theirs, :]
 
         @pl.when(e + LOADS < experts)
         def _():
@@ -235,10 +236,10 @@
 
     @pl.when(~is_end)
     def _():
-        for i in range(total * quarter - max(HELD), total * quarter):
+        for i in range((total - MIDS) * quarter - max(HELD), (total - MIDS) * quarter):
             m = i // quarter
 
-            @pl.when(i >= total * quarter - held)
+            @pl.when(i >= (total - MIDS) * quarter - held)
             def _():
                 send_to(m % 2, m // 2, [far_mid[i % quarter]])
 
@@ -304,27 +305,36 @@
 
 def second_kernel(n, stash, after, land, send, recv):
     group, me = lax.axis_index("expert"), lax.axis_index("shard")
-    is_end, far_end, _, _ = peers(me, n)
+    is_end, far_end, far_mid, _ = peers(me, n)
     quarter = n // 4
     part, rows = stash.shape[1] // quarter, stash.shape[2]
     x = me % quarter
     barrier = pltpu.get_barrier_semaphore()
+    for i in range(quarter):
+        device = jnp.where(is_end, far_end[i], far_mid[i])
+        pl.semaphore_signal(barrier, inc=1, device_id=(group, device), device_id_type=MESH_IDS)
+    pl.semaphore_wait(barrier, quarter)
+
+    def exchange(first, base, start):
+        for i in range(quarter):
+            to = (start + i) % quarter
+            for m in range(first, ENDS):
+                pltpu.make_async_remote_copy(
+                    src_ref=stash.at[m, pl.ds(pl.multiple_of(to * part, part), part), :],
+                    dst_ref=land.at[m, :, pl.ds(pl.multiple_of(x * rows, rows), rows)],
+                    send_sem=send, recv_sem=recv, device_id=(group, base + to), device_id_type=MESH_IDS,
+                ).start()
+        got, sent = land.at[pl.ds(first, ENDS - first)], stash.at[pl.ds(first, ENDS - first)]
+        pltpu.make_async_copy(got, got, recv).wait()
+        pltpu.make_async_copy(sent, sent, send).wait()
 
     @pl.when(is_end)
     def _():
-        for device in far_end:
-            pl.semaphore_signal(barrier, inc=1, device_id=(group, device), device_id_type=MESH_IDS)
-        pl.semaphore_wait(barrier, quarter)
-        for i in range(quarter * SECOND):
-            to, m = i // SECOND, i % SECOND
-            pltpu.make_async_remote_copy(
-                src_ref=stash.at[m, pl.ds(to * part, part), :],
-                dst_ref=land.at[m, :, pl.ds(pl.multiple_of(x * rows, rows), rows)],
-                send_sem=send, recv_sem=recv,
-                device_id=(group, far_end[to]), device_id_type=MESH_IDS,
-            ).start()
-        pltpu.make_async_copy(land, land, recv).wait()
-        pltpu.make_async_copy(stash, stash, send).wait()
+        exchange(0, far_end[0], 0)
+
+    @pl.when(~is_end)
+    def _():
+        exchange(ENDS - MIDS, far_mid[0], x + 1)
 
 
 def second(n, stash, after):
@@ -333,7 +343,7 @@
     anywhere = pl.BlockSpec(memory_space=pl.ANY)
     return pl.pallas_call(
         functools.partial(second_kernel, n),
-        out_shape=pltpu.VMEM((SECOND, span // quarter, quarter * rows), stash.dtype),
+        out_shape=pltpu.VMEM((ENDS, span // quarter, quarter * rows), stash.dtype),
         in_specs=[anywhere, anywhere],
         out_specs=anywhere,
         scratch_shapes=[pltpu.SemaphoreType.DMA, pltpu.SemaphoreType.DMA],
@@ -346,21 +356,28 @@
 
 def fill_kernel(n, gate, up, land, og, ou, done):
     me = lax.axis_index("shard")
-    is_end, _, _, _ = peers(me, n)
-    half, quarter = n // 2, n // 4
+    is_end, far_end, far_mid, _ = peers(me, n)
     experts, width = gate.shape[0], land.shape[2]
-    spot = pl.ds(pl.multiple_of((1 - me // half) * (n - quarter) * (width // quarter), width), width)
-
-    @pl.when(is_end)
-    def _():
+    rows = width // (n // 4)
+
+    def place(first, base):
+        spot = pl.ds(pl.multiple_of(base * rows, width), width)
         copies = []
-        for i in range(SECOND):
-            m = 2 * experts - SECOND + i
+        for i in range(first, ENDS):
+            m = 2 * experts - ENDS + i
             copies.append(pltpu.make_async_copy(land.at[i], (og, ou)[m % 2].at[m // 2, :, spot], done.at[i]))
         for copy in copies:
             copy.start()
         for copy in copies:
             copy.wait()
+
+    @pl.when(is_end)
+    def _():
+        place(0, far_end[0])
+
+    @pl.when(~is_end)
+    def _():
+        place(ENDS - MIDS, far_mid[0])
 
 
 def fill(n, gate, up, land):
@@ -370,7 +387,7 @@
         out_shape=tuple(pltpu.HBM(x.shape, x.dtype) for x in (gate, up)),
         in_specs=[anywhere] * 3,
         out_specs=(anywhere,) * 2,
-        scratch_shapes=[pltpu.SemaphoreType.DMA((SECOND,))],
+        scratch_shapes=[pltpu.SemaphoreType.DMA((ENDS,))],
         input_output_aliases={0: 0, 1: 1},
         compiler_params=pltpu.CompilerParams(vmem_limit_bytes=1024 * 1024),
         name="fill",
@@ -419,7 +436,7 @@
             pltpu.VMEM(final, jnp.bfloat16),
             pltpu.VMEM(final, jnp.bfloat16),
             jax.ShapeDtypeStruct((rows * n, r_cols * groups), jnp.bfloat16),
-            pltpu.VMEM((SECOND, inner // 4, rows), jnp.bfloat16),
+            pltpu.VMEM((ENDS, inner // 4, rows), jnp.bfloat16),
         ),
         in_specs=[anywhere] * 6,
         out_specs=(anywhere, anywhere, pl.BlockSpec(memory_space=pltpu.VMEM), pl.BlockSpec(memory_space=pltpu.VMEM)),
@@ -457,7 +474,7 @@
         r_cols = args[4].shape[1]
         fits = (
             n % 4 == 0 and groups > 1 and rows % 128 == 0 and inner % 128 == 0
-            and (inner // n) % 16 == 0 and r_cols % 16 == 0 and experts % PIECES == 0 and experts > max(SLOTS, LOADS, EARLY) and 2 * SLOTS * (n // 4) > max(HELD) + n // 2
+            and (inner // n) % 16 == 0 and r_cols % 16 == 0 and experts % PIECES == 0 and experts > max(SLOTS, LOADS, EARLY) and 2 * SLOTS * (n // 4) > max(HELD) + (MIDS + 2) * (n // 4) and ENDS >= MIDS
         )
         return fused(n, groups, *args) if fits else plain(*args)
 

time: 548 us -> 548 us (level)
    pallas_call x1, Pallas kernels: 526 us -> 520 us  [fused(): pl.pallas_call(functools.partial(regroup_kernel, n, groups), out_shape=(p...]
where the time goes in v3:
time: 548 us; the launch traced here: 545 us
  Pallas kernels  544 us (99%)
    pallas_call x1, Pallas kernels, fused(): pl.pallas_call(functools.partial(regroup_kernel, n, groups), out_shape=(p...  520 us
    pallas_call x1, Pallas kernels, second(): pl.pallas_call(functools.partial(second_kernel, n), out_shape=pltpu.VMEM(...  14.6 us

profile of v3, /device:TPU:0, one launch (start us, length us, event | category | flops | bytes accessed | tf_op | source)
XLA Modules:
  0.0 544.8 jit_solution(17344072216074262203)
XLA Ops:
  0.6 520.0 %regroup.1 = (bf16[32,96,2048]{2,1,0:T(8,128)(2,1)S(1)}, bf16[32,96,2048]{2,1,0:T(8,128)(2,1)S(1)}, bf16[2048,128]{1,0:T(8,128)(2,1)S(1)}, bf16[6,192,256]{2,1,0:T(8,128)(2,1)S(1)}) custom-call(f32[32,256,768]{2,1,0:T(8,128)} %mg.1, bf16[32,256,768]{2,1,0:T(8,128)(2,1)} %sg.1, f32[32,256,768]{2,1,0:T(8,128)} %mu.1, bf16[32,256,768]{2,1,0:T(8,128)(2,1)} %su.1, ...), custom_call_target="tpu_custom_call" | custom-call | tf_op jit(solution)/shard_map/regroup/pallas_call | solution.py:433
  520.6 8.6 %put.1 = (bf16[32,96,2048]{2,1,0:T(8,128)(2,1)}, bf16[32,96,2048]{2,1,0:T(8,128)(2,1)}, bf16[2048,128]{1,0:T(8,128)(2,1)}, f32[8,128]{1,0:T(8,128)S(1)}) custom-call(bf16[32,96,2048]{2,1,0:T(8,128)(2,1)S(1)} %get-tuple-element.13.gate, bf16[32,96,2048]{2,1,0:T(8,128)(2,1)S(1)} %get-tuple-element.14.up, bf16[2048,128]{1,0:T(8,128)(2,1)S(1)} %get-tuple-element.15.router), custom_call_target="tpu_custom_call" | custom-call | tf_op jit(solution)/shard_map/put/pallas_call | solution.py:416
  529.3 14.6 %second.1.land = bf16[6,96,512]{2,1,0:T(8,128)(2,1)S(1)} custom-call(bf16[6,192,256]{2,1,0:T(8,128)(2,1)S(1)} %get-tuple-element.18.stash, f32[8,128]{1,0:T(8,128)S(1)} %get-tuple-element.19.after), custom_call_target="tpu_custom_call" | custom-call | tf_op jit(solution)/shard_map/second/pallas_call | solution.py:344
  543.9 0.9 fill.1

commit v4 on v3

--- a/solution.py
+++ b/solution.py
@@ -11,7 +11,7 @@
 LOADS = 2
 ENDS = 6
 MIDS = 1
-HELD = (13, 12)
+HELD = (14, 12)
 EARLY = 8
 MESH_IDS = pl.DeviceIdType.MESH
 
@@ -40,6 +40,11 @@
     far_mid = [half - mine * quarter + i for i in range(quarter)]
     near = [mine * half + (place + i) % half for i in range(1, half)]
     return is_end, far_end, far_mid, near
+
+
+def late_pairs(n):
+    blocks = max(MIDS * (n // 4) + max(HELD), ENDS * (n // 4))
+    return -(-blocks // n)
 
 
 def regroup_kernel(n, groups, mg, sg, mu, su, rw, gain, og, ou, orr, stash,
@@ -78,50 +83,66 @@
             pltpu.make_async_copy(gain, gain_v, load_r.at[1]),
         )
 
-    def block(a, e, device):
+    def block(a, e, count, device):
         src = pl.ds(pl.multiple_of(device * part, part), part)
-        return stage.at[a, e % SLOTS, src, :], outs[a].at[e, :, home]
-
-    def send_to(a, e, devices):
+        return stage.at[a, pl.ds(e % SLOTS, count), src, :], outs[a].at[pl.ds(e, count), :, home]
+
+    def send_to(a, e, count, devices):
         for device in devices:
-            src, dst = block(a, e, device)
+            src, dst = block(a, e, count, device)
             pltpu.make_async_remote_copy(
-                src_ref=src, dst_ref=dst, send_sem=send.at[a, e % SLOTS], recv_sem=recv.at[a, e],
+                src_ref=src, dst_ref=dst, send_sem=send.at[a, e // 2 % (SLOTS // 2)], recv_sem=recv.at[a, e // 2],
                 device_id=(group, device), device_id_type=MESH_IDS,
             ).start()
 
-    def seconds_of(a, e):
-        return 2 * e + a >= total - jnp.where(is_end, ENDS, MIDS)
+    def own_copy(a, p):
+        src, dst = block(a, 2 * p, 2, me)
+        return pltpu.make_async_copy(src, dst, own.at[a, p % (SLOTS // 2)])
+
+    def send_pair(a, p):
+        send_to(a, 2 * p, 2, far_end + far_mid + near)
+        own_copy(a, p).start()
 
     def start_sends(a, e, early=False):
         m = 2 * e + a
 
         @pl.when(~is_end | (m < total - ENDS))
         def _():
-            send_to(a, e, far_end)
+            send_to(a, e, 1, far_end)
 
         for i, device in enumerate(far_mid):
             @pl.when(is_end | (x != i if early else m * quarter + i < (total - MIDS) * quarter - held))
             def _():
-                send_to(a, e, [device])
-
-        send_to(a, e, near)
-        src, dst = block(a, e, me)
-        pltpu.make_async_copy(src, dst, own.at[a, e % SLOTS]).start()
-
-    def wait_sends(a, e, blocks=n - 1):
-        many = stage.at[a, e % SLOTS, pl.ds(0, blocks * part), :]
-        pltpu.make_async_copy(many, many, send.at[a, e % SLOTS]).wait()
-        src, dst = block(a, e, me)
-        pltpu.make_async_copy(src, dst, own.at[a, e % SLOTS]).wait()
+                send_to(a, e, 1, [device])
+
+        send_to(a, e, 1, near)
+
+    def send_singles(a, p, early=False):
+        for e in (2 * p, 2 * p + 1):
+            start_sends(a, e, early)
+        own_copy(a, p).start()
+
+    def by_left_out(a, p, wait):
+        first = total - jnp.where(is_end, ENDS, MIDS)
+        for left_out, is_it in enumerate((
+            4 * p + a + 2 < first, (4 * p + a < first) & (4 * p + a + 2 >= first), 4 * p + a >= first,
+        )):
+            @pl.when(is_it)
+            def _():
+                wait(n - 1 - left_out * quarter // 2)
+
+    def wait_sends(a, p, blocks=n - 1):
+        many = stage.at[a, pl.ds(2 * p % SLOTS, 2), pl.ds(0, blocks * part), :]
+        pltpu.make_async_copy(many, many, send.at[a, p % (SLOTS // 2)]).wait()
+        own_copy(a, p).wait()
 
     def merge(a, e):
         for copy in loads(a, e):
             copy.wait()
 
-        @pl.when(e >= SLOTS)
+        @pl.when((e >= SLOTS) & (e % 2 == 0))
         def _():
-            wait_sends(a, e - SLOTS)
+            wait_sends(a, e // 2 - SLOTS // 2)
 
         slot, into = e % LOADS, e % SLOTS
         for c in range(inner // 128):
@@ -175,7 +196,7 @@
     def send_early(a, e):
         @pl.when(~is_end)
         def _():
-            send_to(a, e, [mirror_x])
+            send_to(a, e, 1, [mirror_x])
 
     r_rows = pl.ds(pl.multiple_of(group * r_cols, r_cols), r_cols)
     for m in range(EARLY):
@@ -202,8 +223,9 @@
     def _():
         pl.semaphore_wait(known, 1)
 
-    for m in range(EARLY):
-        start_sends(m % 2, m // 2, early=True)
+    for p in range(EARLY // 4):
+        for a in range(2):
+            send_singles(a, p, early=True)
 
     def hand(src, dst, i, device):
         pltpu.make_async_remote_copy(
@@ -219,20 +241,34 @@
     for device in near:
         hand(r_part, r_all.at[r_rows, home], 1, device)
 
-    merge(0, EARLY // 2)
-    merge(1, EARLY // 2)
-    start_sends(0, EARLY // 2)
-
-    def step(e, carry):
-        merge(0, e)
-        start_sends(1, e - 1)
-        merge(1, e)
-        start_sends(0, e)
+    def merge_pair(a, p):
+        for e in (2 * p, 2 * p + 1):
+            merge(a, e)
+
+    pairs, late = experts // 2, late_pairs(n)
+
+    def step(p, carry):
+        merge_pair(0, p)
+
+        @pl.when(p > EARLY // 4)
+        def _():
+            send_pair(1, p - 1)
+
+        merge_pair(1, p)
+        send_pair(0, p)
         return carry
 
-    lax.fori_loop(EARLY // 2 + 1, experts, step, 0)
-
-    start_sends(1, experts - 1)
+    lax.fori_loop(EARLY // 4, pairs - late, step, 0)
+    send_pair(1, pairs - late - 1)
+
+    def late_step(p, carry):
+        merge_pair(0, p)
+        merge_pair(1, p)
+        send_singles(0, p)
+        send_singles(1, p)
+        return carry
+
+    lax.fori_loop(pairs - late, pairs, late_step, 0)
 
     @pl.when(~is_end)
     def _():
@@ -241,7 +277,7 @@
 
             @pl.when(i >= (total - MIDS) * quarter - held)
             def _():
-                send_to(m % 2, m // 2, [far_mid[i % quarter]])
+                send_to(m % 2, m // 2, 1, [far_mid[i % quarter]])
 
     wait_hands(r_recv, 0, 1)
     mirror = r_all.at[r_rows, pl.ds(pl.multiple_of(mirror_x * rows, rows), rows)]
@@ -272,35 +308,23 @@
         span = slice(c * 128, (c + 1) * 128)
         orr[span, :] = r_all[:, span].astype(jnp.float32).T.astype(jnp.bfloat16)
 
-    def drain(e, carry):
+    def drain(p, carry):
         for a in range(2):
-            @pl.when(seconds_of(a, e))
-            def _():
-                wait_sends(a, e, n - 1 - quarter)
-
-            @pl.when(~seconds_of(a, e))
-            def _():
-                wait_sends(a, e)
+            by_left_out(a, p, functools.partial(wait_sends, a, p))
         return carry
 
-    lax.fori_loop(max(experts - SLOTS, 0), experts, drain, 0)
-
-    def wait_recv(a, e, blocks):
-        many = outs[a].at[e, :, pl.ds(0, blocks * rows)]
-        pltpu.make_async_copy(many, many, recv.at[a, e]).wait()
-
-    def arrive(e, carry):
+    lax.fori_loop(max(pairs - SLOTS // 2, 0), pairs, drain, 0)
+
+    def wait_recv(a, p, blocks):
+        many = outs[a].at[pl.ds(2 * p, 2), :, pl.ds(0, blocks * rows)]
+        pltpu.make_async_copy(many, many, recv.at[a, p]).wait()
+
+    def arrive(p, carry):
         for a in range(2):
-            @pl.when(seconds_of(a, e))
-            def _():
-                wait_recv(a, e, n - 1 - quarter)
-
-            @pl.when(~seconds_of(a, e))
-            def _():
-                wait_recv(a, e, n - 1)
+            by_left_out(a, p, functools.partial(wait_recv, a, p))
         return carry
 
-    lax.fori_loop(0, experts, arrive, 0)
+    lax.fori_loop(0, pairs, arrive, 0)
 
 
 def second_kernel(n, stash, after, land, send, recv):
@@ -449,7 +473,7 @@
             pltpu.VMEM((r_cols, rows), jnp.bfloat16),
             pltpu.VMEM((r_cols * groups, rows * n), jnp.bfloat16),
             dma((2, LOADS)), dma((2, LOADS)), dma((2,)),
-            dma((2, SLOTS)), dma((2, SLOTS)), dma((2, experts)),
+            dma((2, SLOTS // 2)), dma((2, SLOTS // 2)), dma((2, experts // 2)),
             dma((3,)), dma((3,)), dma, dma,
             regular, regular, regular,
         ],
@@ -473,8 +497,9 @@
         experts, rows, inner = args[0].shape
         r_cols = args[4].shape[1]
         fits = (
-            n % 4 == 0 and groups > 1 and rows % 128 == 0 and inner % 128 == 0
-            and (inner // n) % 16 == 0 and r_cols % 16 == 0 and experts % PIECES == 0 and experts > max(SLOTS, LOADS, EARLY) and 2 * SLOTS * (n // 4) > max(HELD) + (MIDS + 2) * (n // 4) and ENDS >= MIDS
+            n % 8 == 0 and groups > 1 and rows % 128 == 0 and inner % 128 == 0
+            and (inner // n) % 16 == 0 and r_cols % 16 == 0 and experts % PIECES == 0 and experts % 2 == 0 and experts // 2 > max(SLOTS // 2, EARLY // 4) + late_pairs(n) and ENDS >= MIDS
+            and late_pairs(n) <= SLOTS // 2
         )
         return fused(n, groups, *args) if fits else plain(*args)
 

time: 548 us -> 547 us (level)
  no operation moved by 1% of the time
where the time goes in v4:
time: 547 us; the launch traced here: 545 us
  Pallas kernels  544 us (99%)
    pallas_call x1, Pallas kernels, fused(): pl.pallas_call(functools.partial(regroup_kernel, n, groups), out_shape=(p...  519 us
    pallas_call x1, Pallas kernels, second(): pl.pallas_call(functools.partial(second_kernel, n), out_shape=pltpu.VMEM(...  15.3 us

profile of v4, /device:TPU:0, one launch (start us, length us, event | category | flops | bytes accessed | tf_op | source)
XLA Modules:
  0.0 544.5 jit_solution(8630520003457071966)
XLA Ops:
  0.6 519.1 %regroup.1 = (bf16[32,96,2048]{2,1,0:T(8,128)(2,1)S(1)}, bf16[32,96,2048]{2,1,0:T(8,128)(2,1)S(1)}, bf16[2048,128]{1,0:T(8,128)(2,1)S(1)}, bf16[6,192,256]{2,1,0:T(8,128)(2,1)S(1)}) custom-call(f32[32,256,768]{2,1,0:T(8,128)} %mg.1, bf16[32,256,768]{2,1,0:T(8,128)(2,1)} %sg.1, f32[32,256,768]{2,1,0:T(8,128)} %mu.1, bf16[32,256,768]{2,1,0:T(8,128)(2,1)} %su.1, ...), custom_call_target="tpu_custom_call" | custom-call | tf_op jit(solution)/shard_map/regroup/pallas_call | solution.py:457
  519.7 8.6 %put.1 = (bf16[32,96,2048]{2,1,0:T(8,128)(2,1)}, bf16[32,96,2048]{2,1,0:T(8,128)(2,1)}, bf16[2048,128]{1,0:T(8,128)(2,1)}, f32[8,128]{1,0:T(8,128)S(1)}) custom-call(bf16[32,96,2048]{2,1,0:T(8,128)(2,1)S(1)} %get-tuple-element.13.gate, bf16[32,96,2048]{2,1,0:T(8,128)(2,1)S(1)} %get-tuple-element.14.up, bf16[2048,128]{1,0:T(8,128)(2,1)S(1)} %get-tuple-element.15.router), custom_call_target="tpu_custom_call" | custom-call | tf_op jit(solution)/shard_map/put/pallas_call | solution.py:440
  528.3 15.3 %second.1.land = bf16[6,96,512]{2,1,0:T(8,128)(2,1)S(1)} custom-call(bf16[6,192,256]{2,1,0:T(8,128)(2,1)S(1)} %get-tuple-element.18.stash, f32[8,128]{1,0:T(8,128)S(1)} %get-tuple-element.19.after), custom_call_target="tpu_custom_call" | custom-call | tf_op jit(solution)/shard_map/second/pallas_call | solution.py:368
  543.7 0.9 fill.1
